TPU v7x, 8 devices: a whole 2x2x1 slice. The times are simulated.
8 devices in a mesh: stage: 2 (over z, y), expert: 4 (over x, core).
Axes of the slice: x: 2, y: 2, z: 1, core: 2. Of those that a mesh axis runs over, the one named last changes fastest.
Arguments:
- x_act: bfloat16 [2, 4096, 2048], P('stage', 'expert')
- route_idx: int32 [2, 4096, 2], P('stage', 'expert')
- route_gate: float32 [2, 4096, 2], P('stage', 'expert')
- w_up: bfloat16 [2, 16, 2048, 1024], P('stage', 'expert')
- w_lin: bfloat16 [2, 16, 2048, 1024], P('stage', 'expert')
- w_down: bfloat16 [2, 16, 1024, 2048], P('stage', 'expert')
- dy_out: bfloat16 [2, 4096, 2048], P('stage', 'expert')
Outputs:
- output 1: bfloat16 [2, 4096, 2048], P('stage', 'expert')
- output 2: bfloat16 [2, 4096, 2048], P('stage', 'expert')
- output 3: bfloat16 [2, 16, 2048, 1024], P('stage', 'expert')
- output 4: bfloat16 [2, 16, 2048, 1024], P('stage', 'expert')
- output 5: bfloat16 [2, 16, 1024, 2048], P('stage', 'expert')
All inputs are finite; a program needn't handle non-finite values.
Results may differ from a plain program's by a relative error of at most 0.00122.
Values are sent between devices in bfloat16 or wider.
A program may use at most 1 GiB of HBM per device.

v0:
```python
import jax
import jax.numpy as jnp
from jax import lax
from jax.sharding import PartitionSpec as P


def slot_matrix(idx_tok, first_expert, num_local, capacity):
    tokens = idx_tok.shape[0]
    expert_ids = first_expert + jnp.arange(num_local, dtype=jnp.int32)
    is_expert = idx_tok[:, :, None] == expert_ids
    member = jnp.sum(is_expert, axis=1).astype(jnp.bfloat16)
    tok_ids = jnp.arange(tokens, dtype=jnp.int32)
    lower_tri = (tok_ids[:, None] > tok_ids[None, :]).astype(jnp.bfloat16)
    earlier = jnp.dot(lower_tri, member, preferred_element_type=jnp.float32).astype(jnp.int32)
    at_slot = earlier[:, :, None] == jnp.arange(capacity, dtype=jnp.int32)
    return (is_expert[:, :, :, None] & at_slot[:, None, :, :]).astype(jnp.bfloat16)


def expert_forward(x_rows, w_up, w_lin, w_down):
    pre_up = jnp.einsum("erd,edf->erf", x_rows, w_up, preferred_element_type=jnp.float32)
    pre_lin = jnp.einsum("erd,edf->erf", x_rows, w_lin, preferred_element_type=jnp.float32)
    act_up = jax.nn.silu(pre_up)
    hidden = (act_up * pre_lin).astype(jnp.bfloat16)
    out_rows = jnp.einsum("erf,efd->erd", hidden, w_down, preferred_element_type=jnp.float32).astype(jnp.bfloat16)
    return out_rows, (pre_up, pre_lin, act_up, hidden)


def expert_backward(x_rows, d_rows, w_up, w_lin, w_down, saved_acts):
    pre_up, pre_lin, act_up, hidden = saved_acts
    d_hidden = jnp.einsum("erd,efd->erf", d_rows, w_down, preferred_element_type=jnp.float32).astype(jnp.bfloat16).astype(jnp.float32)
    sigmoid_up = jax.nn.sigmoid(pre_up)
    d_up = (d_hidden * pre_lin * sigmoid_up * (1.0 + pre_up * (1.0 - sigmoid_up))).astype(jnp.bfloat16)
    d_lin = (d_hidden * act_up).astype(jnp.bfloat16)
    g_up = jnp.einsum("erd,erf->edf", x_rows, d_up, preferred_element_type=jnp.float32).astype(jnp.bfloat16)
    g_lin = jnp.einsum("erd,erf->edf", x_rows, d_lin, preferred_element_type=jnp.float32).astype(jnp.bfloat16)
    g_down = jnp.einsum("erf,erd->efd", hidden, d_rows, preferred_element_type=jnp.float32).astype(jnp.bfloat16)
    dx_rows = (jnp.einsum("erf,edf->erd", d_up, w_up, preferred_element_type=jnp.float32) + jnp.einsum("erf,edf->erd", d_lin, w_lin, preferred_element_type=jnp.float32)).astype(jnp.bfloat16)
    return dx_rows, g_up, g_lin, g_down


def solution(mesh):
    stages = mesh.shape["stage"]
    groups = mesh.shape["expert"]
    send_next = [(src, (src + 1) % stages) for src in range(stages)]
    send_back = [(src, (src - 1) % stages) for src in range(stages)]
    tok_spec = P("stage", "expert", None)
    w_spec = P("stage", "expert", None, None)

    def to_experts(slot_rows):
        num_experts, capacity, row_width = slot_rows.shape
        split_rows = slot_rows.reshape(groups, num_experts // groups, capacity, row_width)
        return lax.all_to_all(split_rows, "expert", 0, 2, tiled=True)[0]

    def to_owners(expert_rows):
        local_exp, gathered, row_width = expert_rows.shape
        back_rows = lax.all_to_all(expert_rows[None], "expert", 2, 0, tiled=True)
        return back_rows.reshape(groups * local_exp, gathered // groups, row_width)

    def device_step(x_act, route_idx, route_gate, w_up, w_lin, w_down, dy_out):
        tokens = x_act.shape[1]
        num_experts = w_up.shape[1] * groups
        capacity = 4 * tokens // num_experts
        x_tok = lax.ppermute(x_act[0], "stage", send_next)
        idx_tok = lax.ppermute(route_idx[0], "stage", send_next)
        gate_tok = lax.ppermute(route_gate[0], "stage", send_next)
        slot_place = slot_matrix(idx_tok, 0, num_experts, capacity)
        x_send = jnp.einsum("tjec,td->ecd", slot_place, x_tok, preferred_element_type=jnp.float32).astype(jnp.bfloat16)
        x_rows = to_experts(x_send)
        out_rows, saved_acts = expert_forward(x_rows, w_up[0], w_lin[0], w_down[0])
        out_copies = jnp.einsum("tjec,ecd->tjd", slot_place, to_owners(out_rows), preferred_element_type=jnp.float32)
        y_tok = jnp.sum(gate_tok[:, :, None] * out_copies, axis=1).astype(jnp.bfloat16)
        d_copies = (gate_tok[:, :, None] * dy_out[0][:, None, :].astype(jnp.float32)).astype(jnp.bfloat16)
        d_send = jnp.einsum("tjec,tjd->ecd", slot_place, d_copies, preferred_element_type=jnp.float32).astype(jnp.bfloat16)
        d_rows = to_experts(d_send)
        dx_rows, g_up, g_lin, g_down = expert_backward(x_rows, d_rows, w_up[0], w_lin[0], w_down[0], saved_acts)
        dx_tok = jnp.einsum("tjec,ecd->td", slot_place, to_owners(dx_rows), preferred_element_type=jnp.float32).astype(jnp.bfloat16)
        dx_prev = lax.ppermute(dx_tok, "stage", send_back)
        return y_tok[None], dx_prev[None], g_up[None], g_lin[None], g_down[None]

    return jax.shard_map(device_step, mesh=mesh, in_specs=(tok_spec, tok_spec, tok_spec, w_spec, w_spec, w_spec, tok_spec), out_specs=(tok_spec, tok_spec, w_spec, w_spec, w_spec), check_vma=False)
```

profile of v0, /device:TPU:0, one launch (start us, length us, event | category | flops | bytes accessed | tf_op | source)
XLA Modules:
  0.0 1045.8 jit_solution(12908684433337106500)
XLA Ops:
  23.7 39.9 %bitcast_convert_fusion = bf16[16,256,2048]{2,1,0:T(8,128)(2,1)} fusion(pred[1024,16,256]{0,2,1:T(8,128)(4,1)} %iota_compare_fusion, pred[1024,2,16]{0,1,2:T(4,128)(4,1)S(1)} %iota_compare_fusion.5, bf16[1024,2,2048,1]{2,0,1,3:T(8,128)(2,1)} %fusion.70), kind=kOutput, calls=%fused_computation.5 | convolution fusion | flops 34376515584 | bytes 29392896 | tf_op jit(solution)/shard_map/tjec,tjd->ecd/dot_general | solution.py:73
  73.1 11.7 %convert_reduce_fusion = bf16[1024,16,256]{0,2,1:T(8,128)(2,1)} fusion(pred[1024,16,256]{0,2,1:T(8,128)(4,1)} %iota_compare_fusion, pred[1024,2,16]{0,1,2:T(4,128)(4,1)S(1)} %iota_compare_fusion.5), kind=kLoop, calls=%fused_computation.7 | loop fusion | flops 29360128 | bytes 12615680 | tf_op jit(solution)/shard_map/tjec,td->ecd/reduce_sum | solution.py:67
  84.7 79.6 %collective-permute-done.2 = bf16[1024,2048]{1,0:T(8,128)(2,1)} collective-permute-done((bf16[1024,2048]{1,0:T(8,128)(2,1)}, bf16[1024,2048]{1,0:T(8,128)(2,1)}, u32[]{:S(2)}, u32[]{:S(2)}) %collective-permute-start.2) | collective-permute-done | bytes 4194336 | tf_op jit(solution)/shard_map/ppermute | solution.py:63
  164.3 24.7 %convolution_convert_fusion = bf16[16,256,2048]{2,1,0:T(8,128)(2,1)} fusion(bf16[1024,16,256]{0,2,1:T(8,128)(2,1)} %convert_reduce_fusion, bf16[1024,2048]{1,0:T(8,128)(2,1)} %collective-permute-done.2), kind=kOutput, calls=%fused_computation.40 | convolution fusion | flops 17179869184 | bytes 29360128 | tf_op jit(solution)/shard_map/tjec,td->ecd/dot_general | solution.py:67
  189.0 64.8 %all-to-all-done.2 = bf16[4,4,256,2048]{3,2,1,0:T(8,128)(2,1)} async-done(((bf16[4,4,256,2048]{3,2,1,0:T(8,128)(2,1)}), bf16[4,4,256,2048]{3,2,1,0:T(8,128)(2,1)}, u32[]{:S(2)}, u32[]{:S(2)}) %all-to-all-start.2) | async-done | bytes 16777248 | tf_op jit(solution)/shard_map/all_to_all | solution.py:52
  260.9 14.2 %copy.25 = bf16[1,4,4,256,2048]{4,3,2,1,0:T(8,128)(2,1)} copy(bf16[1,4,4,256,2048]{4,3,1,2,0:T(8,128)(2,1)} %bitcast.25) | data formatting | bytes 33554432 | tf_op jit(solution)/shard_map/all_to_all | solution.py:52
  275.1 26.6 %fusion.36 = bf16[4,1024,1024]{2,1,0:T(8,128)(2,1)} fusion(bf16[4,1024,2048]{2,1,0:T(8,128)(2,1)} %bitcast.107, bf16[1,4,1024,2048]{3,2,1,0:T(8,128)(2,1)} %param.12), kind=kOutput, calls=%fused_computation.46 | convolution fusion | flops 17184063488 | bytes 41943040 | tf_op jit(solution)/shard_map/erd,efd->erf/dot_general | solution.py:30
  301.7 141.9 %all-to-all-done = bf16[4,4,256,2048]{3,2,1,0:T(8,128)(2,1)} async-done(((bf16[4,4,256,2048]{3,2,1,0:T(8,128)(2,1)}), bf16[4,4,256,2048]{3,2,1,0:T(8,128)(2,1)}, u32[]{:S(2)}, u32[]{:S(2)}) %all-to-all-start) | async-done | bytes 16777248 | tf_op jit(solution)/shard_map/all_to_all | solution.py:52
  457.4 22.3 %fusion.20 = f32[4,1024,1024]{2,1,0:T(8,128)} fusion(bf16[4,1024,2048]{2,1,0:T(8,128)(2,1)S(1)} %bitcast.103, bf16[1,4,2048,1024]{3,2,1,0:T(8,128)(2,1)} %param.10), kind=kOutput, calls=%fused_computation.25 | convolution fusion | flops 17179869184 | bytes 50331648 | tf_op jit(solution)/shard_map/erd,edf->erf/dot_general | solution.py:20
  479.7 34.0 %fusion.8 = (bf16[4,1024,1024]{2,1,0:T(8,128)(2,1)}, bf16[4,1024,1024]{2,1,0:T(8,128)(2,1)}) fusion(bf16[4,1024,1024]{2,1,0:T(8,128)(2,1)} %fusion.36, f32[4,1024,1024]{2,1,0:T(8,128)} %fusion.20, bf16[4,1024,2048]{2,1,0:T(8,128)(2,1)} %bitcast.104, bf16[1,4,2048,1024]{3,2,1,0:T(8,128)(2,1)} %param.11), kind=kOutput, calls=%fused_computation.12 | convolution fusion | flops 17238589440 | bytes 75497472 | tf_op jit(solution)/shard_map/erd,edf->erf/dot_general | solution.py:21
  513.7 26.7 %fusion.18 = f32[4,1024,2048]{2,1,0:T(8,128)} fusion(bf16[4,1024,1024]{2,1,0:T(8,128)(2,1)} %get-tuple-element.5, bf16[1,4,2048,1024]{3,2,1,0:T(8,128)(2,1)} %param.10), kind=kOutput, calls=%fused_computation.23 | convolution fusion | flops 17179869184 | bytes 58720256 | tf_op jit(solution)/shard_map/erf,edf->erd/dot_general | solution.py:37
  540.5 36.0 %fusion.29 = bf16[1,4,1024,2048]{3,2,1,0:T(8,128)(2,1)} fusion(f32[4,1024,2048]{2,1,0:T(8,128)} %fusion.18, bf16[1,4,2048,1024]{3,2,1,0:T(8,128)(2,1)} %param.11, bf16[4,1024,1024]{2,1,0:T(8,128)(2,1)} %fusion.36, f32[4,1024,1024]{2,1,0:T(8,128)} %fusion.20), kind=kOutput, calls=%fused_computation.41 | convolution fusion | flops 17226006528 | bytes 92274688 | tf_op jit(solution)/shard_map/erf,edf->erd/dot_general | solution.py:37
  576.5 22.5 %copy.26 = bf16[1,4,1024,2048]{3,1,0,2:T(4,128)(2,1)} copy(bf16[1,4,1024,2048]{3,2,1,0:T(8,128)(2,1)} %fusion.29) | data formatting | bytes 33554432 | tf_op jit(solution)/shard_map/broadcast_in_dim | solution.py:56
  606.1 27.2 %convert_bitcast_fusion.3 = bf16[1,4,1024,2048]{3,2,1,0:T(8,128)(2,1)} fusion(bf16[4,1024,1024]{2,1,0:T(8,128)(2,1)} %get-tuple-element.6, bf16[1,4,1024,2048]{3,2,1,0:T(8,128)(2,1)} %param.12), kind=kOutput, calls=%fused_computation.31 | convolution fusion | flops 17188257792 | bytes 41943040 | tf_op jit(solution)/shard_map/erf,efd->erd/dot_general | solution.py:24
  633.3 22.1 %copy.22 = bf16[1,4,1024,2048]{3,1,0,2:T(4,128)(2,1)} copy(bf16[1,4,1024,2048]{3,2,1,0:T(8,128)(2,1)} %convert_bitcast_fusion.3) | data formatting | bytes 33554432 | tf_op jit(solution)/shard_map/broadcast_in_dim | solution.py:56
  655.4 133.4 %all-to-all-done.3 = bf16[1,4,1024,2048]{3,1,0,2:T(4,128)(2,1)} async-done(((bf16[1,4,1024,2048]{3,1,0,2:T(4,128)(2,1)}), bf16[1,4,1024,2048]{3,1,0,2:T(4,128)(2,1)}, u32[]{:S(2)}, u32[]{:S(2)}) %all-to-all-start.3) | async-done | bytes 16777248 | tf_op jit(solution)/shard_map/all_to_all | solution.py:56
  796.0 31.1 %convert_bitcast_fusion.1 = bf16[1,4,2048,1024]{3,2,1,0:T(8,128)(2,1)} fusion(bf16[4,1024,2048]{2,1,0:T(8,128)(2,1)} %bitcast.105, bf16[4,1024,1024]{2,1,0:T(8,128)(2,1)} %fusion.36, f32[4,1024,1024]{2,1,0:T(8,128)} %fusion.20), kind=kOutput, calls=%fused_computation.28 | convolution fusion | flops 17217617920 | bytes 58720256 | tf_op jit(solution)/shard_map/erd,erf->edf/dot_general | solution.py:35
  827.0 26.6 %convert_bitcast_fusion = bf16[1,4,1024,2048]{3,2,1,0:T(8,128)(2,1)} fusion(bf16[4,1024,1024]{2,1,0:T(8,128)(2,1)} %get-tuple-element.6, bf16[4,1024,2048]{2,1,0:T(8,128)(2,1)} %bitcast.108), kind=kOutput, calls=%fused_computation.27 | convolution fusion | flops 17188257792 | bytes 41943040 | tf_op jit(solution)/shard_map/erf,erd->efd/dot_general | solution.py:36
  853.6 15.2 %copy.27 = bf16[1,4,4,256,2048]{4,3,1,2,0:T(8,128)(2,1)S(1)} copy(bf16[1,4,4,256,2048]{4,1,3,2,0:T(4,128)(2,1)} %bitcast.28) | data formatting | bytes 33554432 | tf_op jit(solution)/shard_map/all_to_all | solution.py:56
  868.8 21.3 %bitcast_convert_fusion.1 = bf16[1024,2048]{1,0:T(8,128)(2,1)} fusion(bf16[1024,16,256]{0,2,1:T(8,128)(2,1)} %convert_reduce_fusion, bf16[16,256,2048]{2,1,0:T(8,128)(2,1)S(1)} %bitcast.112), kind=kOutput, calls=%fused_computation.43 | convolution fusion | flops 17179869184 | bytes 29360128 | tf_op jit(solution)/shard_map/tjec,ecd->td/dot_general | solution.py:76
  892.1 24.1 %convert_bitcast_fusion.2 = bf16[1,4,2048,1024]{3,2,1,0:T(8,128)(2,1)} fusion(bf16[4,1024,2048]{2,1,0:T(8,128)(2,1)} %bitcast.106, bf16[4,1024,1024]{2,1,0:T(8,128)(2,1)S(1)} %bitcast.118), kind=kOutput, calls=%fused_computation.29 | convolution fusion | flops 17188257792 | bytes 41943040 | tf_op jit(solution)/shard_map/erd,erf->edf/dot_general | solution.py:34
  916.1 62.5 %all-to-all-done.1 = bf16[1,4,1024,2048]{3,1,0,2:T(4,128)(2,1)} async-done(((bf16[1,4,1024,2048]{3,1,0,2:T(4,128)(2,1)}), bf16[1,4,1024,2048]{3,1,0,2:T(4,128)(2,1)}, u32[]{:S(2)}, u32[]{:S(2)}) %all-to-all-start.1) | async-done | bytes 16777248 | tf_op jit(solution)/shard_map/all_to_all | solution.py:56
  978.7 18.8 %copy.23 = bf16[1,4,4,256,2048]{4,3,1,2,0:T(8,128)(2,1)} copy(bf16[1,4,4,256,2048]{4,1,3,2,0:T(4,128)(2,1)} %bitcast.12) | data formatting | bytes 33554432 | tf_op jit(solution)/shard_map/all_to_all | solution.py:56
  997.4 43.1 %fusion.10 = bf16[1024,2048]{1,0:T(8,128)(2,1)} fusion(f32[1024,2]{0,1:T(2,128)S(1)} %copy-done.5, bf16[16,256,2048,1]{2,1,3,0:T(8,128)(2,1)} %bitcast.111, pred[1024,16,256]{0,2,1:T(8,128)(4,1)S(1)} %copy-done, pred[1024,2,16]{0,1,2:T(4,128)(4,1)S(1)} %copy-done.3), kind=kOutput, calls=%fused_computation.15 | convolution fusion | flops 34374418432 | bytes 25206784 | tf_op jit(solution)/shard_map/tjec,ecd->tjd/dot_general | solution.py:70
  (36 shorter events, 74.4 us)
Async XLA Ops:
  0.6 10.1 collective-permute-start.1
  4.0 11.9 %collective-permute-start = (f32[1024,2]{0,1:T(2,128)}, f32[1024,2]{0,1:T(2,128)S(1)}, u32[]{:S(2)}, u32[]{:S(2)}) collective-permute-start(f32[1024,2]{0,1:T(2,128)} %bitcast.115), channel_id=1, source_target_pairs={{0,4},{4,0},{1,5},{5,1},{2,6},{6,2},{3,7},{7,3}} | collective-permute-start | bytes 24584 | tf_op jit(solution)/shard_map/ppermute | solution.py:65
  15.9 57.2 %copy-start.2 = (pred[1024,2,16]{0,1,2:T(4,128)(4,1)}, pred[1024,2,16]{0,1,2:T(4,128)(4,1)S(1)}, u32[]{:S(2)}) copy-start(pred[1024,2,16]{0,1,2:T(4,128)(4,1)S(1)} %iota_compare_fusion.5) | copy-start | bytes 98308
  15.9 47.7 %copy-start.4 = (f32[1024,2]{0,1:T(2,128)}, f32[1024,2]{0,1:T(2,128)S(1)}, u32[]{:S(2)}) copy-start(f32[1024,2]{0,1:T(2,128)S(1)} %collective-permute-done) | copy-start | bytes 24580
  63.6 190.1 %all-to-all-start.2 = ((bf16[4,4,256,2048]{3,2,1,0:T(8,128)(2,1)}), bf16[4,4,256,2048]{3,2,1,0:T(8,128)(2,1)}, u32[]{:S(2)}, u32[]{:S(2)}) async-start(bf16[4,4,256,2048]{3,2,1,0:T(8,128)(2,1)} %bitcast.109), calls=%async_computation.2 | async-start | bytes 33554432 | tf_op jit(solution)/shard_map/all_to_all | solution.py:52
  71.1 93.2 %collective-permute-start.2 = (bf16[1024,2048]{1,0:T(8,128)(2,1)}, bf16[1024,2048]{1,0:T(8,128)(2,1)}, u32[]{:S(2)}, u32[]{:S(2)}) collective-permute-start(bf16[1024,2048]{1,0:T(8,128)(2,1)} %bitcast.113), channel_id=1, source_target_pairs={{0,4},{4,0},{1,5},{5,1},{2,6},{6,2},{3,7},{7,3}} | collective-permute-start | bytes 12582920 | tf_op jit(solution)/shard_map/ppermute | solution.py:63
  253.8 189.9 %all-to-all-start = ((bf16[4,4,256,2048]{3,2,1,0:T(8,128)(2,1)}), bf16[4,4,256,2048]{3,2,1,0:T(8,128)(2,1)}, u32[]{:S(2)}, u32[]{:S(2)}) async-start(bf16[4,4,256,2048]{3,2,1,0:T(8,128)(2,1)} %bitcast.110), calls=%async_computation | async-start | bytes 33554432 | tf_op jit(solution)/shard_map/all_to_all | solution.py:52
  451.7 5.7 copy-start.1
  599.0 189.8 %all-to-all-start.3 = ((bf16[1,4,1024,2048]{3,1,0,2:T(4,128)(2,1)}), bf16[1,4,1024,2048]{3,1,0,2:T(4,128)(2,1)}, u32[]{:S(2)}, u32[]{:S(2)}) async-start(bf16[1,4,1024,2048]{3,1,0,2:T(4,128)(2,1)} %copy.26), calls=%async_computation.3 | async-start | bytes 33554432 | tf_op jit(solution)/shard_map/all_to_all | solution.py:56
  788.8 189.9 %all-to-all-start.1 = ((bf16[1,4,1024,2048]{3,1,0,2:T(4,128)(2,1)}), bf16[1,4,1024,2048]{3,1,0,2:T(4,128)(2,1)}, u32[]{:S(2)}, u32[]{:S(2)}) async-start(bf16[1,4,1024,2048]{3,1,0,2:T(4,128)(2,1)} %copy.22), calls=%async_computation.1 | async-start | bytes 33554432 | tf_op jit(solution)/shard_map/all_to_all | solution.py:56
  853.6 38.4 %slice-start = ((s8[8388608]{0:T(1024)(128)(4,1)}), s8[4194304]{0:T(1024)(128)(4,1)S(1)}, s32[]{:S(2)}) async-start(s8[8388608]{0:T(1024)(128)(4,1)} %bitcast.117), calls=%async_computation.4 | async-start | bytes 8388608
  868.8 23.2 %slice-start.1 = ((s8[8388608]{0:T(1024)(128)(4,1)}), s8[4194304]{0:T(1024)(128)(4,1)S(1)}, s32[]{:S(2)}) async-start(s8[8388608]{0:T(1024)(128)(4,1)} %bitcast.117), calls=%async_computation.5 | async-start | bytes 8388608
  890.1 150.5 %collective-permute-start.3 = (bf16[1024,2048]{1,0:T(8,128)(2,1)}, bf16[1024,2048]{1,0:T(8,128)(2,1)}, u32[]{:S(2)}, u32[]{:S(2)}) collective-permute-start(bf16[1024,2048]{1,0:T(8,128)(2,1)} %bitcast_convert_fusion.1), channel_id=1, source_target_pairs={{0,4},{4,0},{1,5},{5,1},{2,6},{6,2},{3,7},{7,3}} | collective-permute-start | bytes 12582920 | tf_op jit(solution)/shard_map/ppermute | solution.py:77
  978.7 18.8 %copy-start = (pred[1024,16,256]{0,2,1:T(8,128)(4,1)S(1)}, pred[1024,16,256]{0,2,1:T(8,128)(4,1)}, u32[]{:S(2)}) copy-start(pred[1024,16,256]{0,2,1:T(8,128)(4,1)} %iota_compare_fusion) | copy-start | bytes 12582916
  978.7 18.8 %copy-start.3 = (pred[1024,2,16]{0,1,2:T(4,128)(4,1)S(1)}, pred[1024,2,16]{0,1,2:T(4,128)(4,1)}, u32[]{:S(2)}) copy-start(pred[1024,2,16]{0,1,2:T(4,128)(4,1)} %copy-done.2) | copy-start | bytes 98308
  978.7 18.8 %copy-start.5 = (f32[1024,2]{0,1:T(2,128)S(1)}, f32[1024,2]{0,1:T(2,128)}, u32[]{:S(2)}) copy-start(f32[1024,2]{0,1:T(2,128)} %copy-done.4) | copy-start | bytes 24580
where the time goes:
time: 1050 us
  waiting for transfers between devices  482 us (46%)
  matrix products  384 us (37%)
  local copies, waits for them, and re-layouts  111 us (11%)
  starting transfers between devices  36.2 us (3%)
  other arithmetic  30.8 us (3%)
    all_to_all x2, waiting for transfers between devices, to_experts(): return lax.all_to_all(split_rows, 'expert', 0, 2, tiled=True)[0]  207 us
    all_to_all x2, waiting for transfers between devices, to_owners(): back_rows = lax.all_to_all(expert_rows[None], 'expert', 2, 0, tiled=True)  196 us
    ppermute x1, waiting for transfers between devices, device_step(): x_tok = lax.ppermute(x_act[0], 'stage', send_next)  79.6 us
    broadcast_in_dim x2, local copies, waits for them, and re-layouts, to_owners(): back_rows = lax.all_to_all(expert_rows[None], 'expert', 2, 0, tiled=True)  44.7 us
    dot_general x1, matrix products, device_step(): jnp.einsum('tjec,ecd->tjd', slot_place, to_owners(out_rows), preferred_el...  43.1 us
    dot_general x1, matrix products, device_step(): jnp.einsum('tjec,tjd->ecd', slot_place, d_copies, preferred_element_type=...  39.9 us
    dot_general x1, matrix products, expert_backward(): jnp.einsum('erf,edf->erd', d_lin, w_lin, preferred_element_type=jnp.float32)  36 us
    dot_general x1, matrix products, expert_forward(): jnp.einsum('erd,edf->erf', x_rows, w_lin, preferred_element_type=jnp.floa...  34 us
  transfers between devices with their start and end apart: 8, of which 5 were waited for; matrix products, arithmetic and copies ran while one was open for 30% of the time, Pallas kernels for 0%

commit v1 on v0

v1 whole, which is shorter than its diff:
```python
import functools

import jax
import jax.numpy as jnp
from jax import lax
from jax.experimental import pallas as pl
from jax.experimental.pallas import tpu as pltpu
from jax.sharding import PartitionSpec as P


F32 = jnp.float32
BF16 = jnp.bfloat16
NT = (((1,), (1,)), ((), ()))
TN = (((0,), (0,)), ((), ()))


def mm(a, b, dims=(((1,), (0,)), ((), ()))):
    return lax.dot_general(a, b, dims, preferred_element_type=F32)


def call(body, grid, in_specs, out_specs, out_shape, args, flops, scratch=()):
    nbytes = sum(a.size * a.dtype.itemsize for a in args)
    return pl.pallas_call(
        body, grid=grid, in_specs=in_specs, out_specs=out_specs, out_shape=out_shape,
        scratch_shapes=list(scratch),
        cost_estimate=pl.CostEstimate(flops=flops, bytes_accessed=nbytes, transcendentals=0),
        compiler_params=pltpu.CompilerParams(dimension_semantics=("arbitrary",) * len(grid)),
    )(*args)


def spec(block, index):
    return pl.BlockSpec(block, index)


def dispatch_body(*refs, sizes, scale):
    count = sum(len(per) for per in sizes)
    pos_ref, gate_ref = refs[:2]
    chunks, (out_ref, hit_ref, scale_ref) = refs[2:2 + count], refs[2 + count:]
    num_exp, cap = out_ref.shape[0], out_ref.shape[1] // 2
    tokens = pos_ref.shape[3]

    @pl.when(pl.program_id(0) == 0)
    def _():
        slot = lax.broadcasted_iota(jnp.int32, (cap, tokens), 0)
        for s in range(2):
            for e in range(num_exp):
                hit = pos_ref[s, e] == slot
                hit_ref[s, e * cap:(e + 1) * cap, :] = hit.astype(BF16)
                if scale:
                    scale_ref[s, e * cap:(e + 1) * cap, :] = jnp.sum(jnp.where(hit, gate_ref[s, e], 0.0), axis=1, keepdims=True)

    at = 0
    for s, per in enumerate(sizes):
        rows, first = None, 0
        for size in per:
            part = mm(hit_ref[s][:, first:first + size], chunks[at][...])
            rows = part if rows is None else rows + part
            first, at = first + size, at + 1
        if scale:
            rows = rows * scale_ref[s]
        rows = rows.astype(BF16)
        for e in range(num_exp):
            out_ref[e, s * cap:(s + 1) * cap, :] = rows[e * cap:(e + 1) * cap]


def dispatch(pos, gate, blocks, cap, scale):
    _, num_exp, _, tokens = pos.shape
    chunks = [c for blk in blocks for c in blk]
    sizes = tuple(tuple(c.shape[0] for c in blk) for blk in blocks)
    width = chunks[0].shape[1]
    dt = 512
    row = spec(pos.shape, lambda d: (0, 0, 0, 0))
    toks = [spec((c.shape[0], dt), lambda d: (0, d)) for c in chunks]
    return call(functools.partial(dispatch_body, sizes=sizes, scale=scale), (width // dt,), [row, row] + toks,
                spec((num_exp, 2 * cap, dt), lambda d: (0, 0, d)),
                jax.ShapeDtypeStruct((num_exp, 2 * cap, width), BF16), (pos, gate, *chunks),
                4 * cap * tokens * width * num_exp,
                [pltpu.VMEM((2, num_exp * cap, tokens), BF16), pltpu.VMEM((2, num_exp * cap, 1), F32)])


def forward_body(x_ref, wu_ref, wl_ref, a_ref, b_ref, h_ref):
    a = mm(x_ref[0], wu_ref[0])
    b = mm(x_ref[0], wl_ref[0])
    a_ref[0] = a
    b_ref[0] = b
    h_ref[0] = (jax.nn.silu(a) * b).astype(BF16)


def forward(x_rows, w_up, w_lin):
    num_exp, rows, width = x_rows.shape
    ff = w_up.shape[2]
    ft = 512
    w = spec((1, width, ft), lambda e, f: (e, 0, f))
    o = spec((1, rows, ft), lambda e, f: (e, 0, f))
    full = functools.partial(jax.ShapeDtypeStruct, (num_exp, rows, ff))
    return call(forward_body, (num_exp, ff // ft), [spec((1, rows, width), lambda e, f: (e, 0, 0)), w, w], [o, o, o],
                [full(F32), full(F32), full(BF16)], (x_rows, w_up, w_lin), 4 * num_exp * rows * width * ff)


def act_grads(a, b, dh):
    sig = jax.nn.sigmoid(a)
    d_up = (dh * b * sig * (1.0 + a * (1.0 - sig))).astype(BF16)
    d_lin = (dh * (a * sig)).astype(BF16)
    return d_up, d_lin


def backward_body(u_ref, wd_ref, a_ref, b_ref, da_ref, db_ref):
    dh = mm(u_ref[0], wd_ref[0], NT).astype(BF16).astype(F32)
    da_ref[0], db_ref[0] = act_grads(a_ref[0], b_ref[0], dh)


def backward(u_rows, w_down, a, b):
    num_exp, rows, width = u_rows.shape
    ff = w_down.shape[1]
    ft = 512
    o = spec((1, rows, ft), lambda e, f: (e, 0, f))
    full = jax.ShapeDtypeStruct((num_exp, rows, ff), BF16)
    return call(backward_body, (num_exp, ff // ft),
                [spec((1, rows, width), lambda e, f: (e, 0, 0)), spec((1, ft, width), lambda e, f: (e, f, 0)), o, o], [o, o],
                [full, full], (u_rows, w_down, a, b), 2 * num_exp * rows * width * ff)


def both_body(x_ref, u_ref, wu_ref, wl_ref, wd_ref, h_ref, da_ref, db_ref):
    a = mm(x_ref[0], wu_ref[0])
    b = mm(x_ref[0], wl_ref[0])
    h_ref[0] = (jax.nn.silu(a) * b).astype(BF16)
    dh = mm(u_ref[0], wd_ref[0], NT).astype(BF16).astype(F32)
    da_ref[0], db_ref[0] = act_grads(a, b, dh)


def both(x_rows, u_rows, w_up, w_lin, w_down):
    num_exp, rows, width = x_rows.shape
    ff = w_up.shape[2]
    ft = 512
    r = spec((1, rows, width), lambda e, f: (e, 0, 0))
    w = spec((1, width, ft), lambda e, f: (e, 0, f))
    o = spec((1, rows, ft), lambda e, f: (e, 0, f))
    full = jax.ShapeDtypeStruct((num_exp, rows, ff), BF16)
    return call(both_body, (num_exp, ff // ft), [r, r, w, w, spec((1, ft, width), lambda e, f: (e, f, 0))], [o, o, o],
                [full, full, full], (x_rows, u_rows, w_up, w_lin, w_down), 6 * num_exp * rows * width * ff)


def out_body(two_ref, pos_ref, coef_ref, h_ref, wd_ref, ya_ref, yb_ref, place_ref, rows_ref):
    num_exp, rows, _ = h_ref.shape
    cap = rows // 2
    tokens = ya_ref.shape[0]

    def build(s, j):
        slot = lax.broadcasted_iota(jnp.int32, (tokens, cap), 1)
        for e in range(num_exp):
            at = pos_ref[s][:, j * num_exp + e:j * num_exp + e + 1]
            place_ref[s, j * tokens:(j + 1) * tokens, e * cap:(e + 1) * cap] = (at == slot).astype(BF16)

    @pl.when(pl.program_id(0) == 0)
    def _():
        for s in range(2):
            build(s, 0)
            pl.when(two_ref[s] > 0)(functools.partial(build, s, 1))

    for e in range(num_exp):
        o = mm(h_ref[e], wd_ref[e]).astype(BF16)
        for s in range(2):
            rows_ref[s, e * cap:(e + 1) * cap, :] = o[s * cap:(s + 1) * cap]
    for s, y_ref in enumerate((ya_ref, yb_ref)):

        @pl.when(two_ref[s] == 0)
        def _():
            y_ref[...] = mm(place_ref[s, :tokens], rows_ref[s]).astype(BF16)

        @pl.when(two_ref[s] > 0)
        def _():
            first = coef_ref[s][:, 0:1] * mm(place_ref[s, :tokens], rows_ref[s])
            y_ref[...] = (first + coef_ref[s][:, 1:2] * mm(place_ref[s, tokens:], rows_ref[s])).astype(BF16)


def out_rows(two, pos, coef, hidden, w_down, part, parts):
    _, tokens, _ = pos.shape
    num_exp, rows, ff = hidden.shape
    width = w_down.shape[2] // parts
    dt = 256
    first = part * (width // dt)
    whole = lambda arr: spec(arr.shape, lambda d: (0,) * arr.ndim)
    o = spec((tokens, dt), lambda d: (0, d))
    full = jax.ShapeDtypeStruct((tokens, width), BF16)
    return call(out_body, (width // dt,),
                [pl.BlockSpec(memory_space=pltpu.SMEM), whole(pos), whole(coef), whole(hidden),
                 spec((num_exp, ff, dt), lambda d: (0, 0, first + d))], [o, o],
                [full, full], (two, pos, coef, hidden, w_down),
                2 * num_exp * rows * ff * width + 8 * tokens * num_exp * (rows // 2) * width,
                [pltpu.VMEM((2, 2 * tokens, num_exp * (rows // 2)), BF16), pltpu.VMEM((2, num_exp * (rows // 2), dt), BF16)])


def dx_body(pos_ref, da_ref, db_ref, wu_ref, wl_ref, ya_ref, yb_ref, place_ref, rows_ref):
    num_exp, rows, _ = da_ref.shape
    cap = rows // 2
    tokens = ya_ref.shape[0]

    @pl.when(pl.program_id(0) == 0)
    def _():
        slot = lax.broadcasted_iota(jnp.int32, (tokens, cap), 1)
        for s in range(2):
            for e in range(num_exp):
                at = pos_ref[s][:, e:e + 1]
                place_ref[s, :, e * cap:(e + 1) * cap] = (at == slot).astype(BF16)

    for e in range(num_exp):
        o = (mm(da_ref[e], wu_ref[e], NT) + mm(db_ref[e], wl_ref[e], NT)).astype(BF16)
        for s in range(2):
            rows_ref[s, e * cap:(e + 1) * cap, :] = o[s * cap:(s + 1) * cap]
    for s, y_ref in enumerate((ya_ref, yb_ref)):
        y_ref[...] = mm(place_ref[s], rows_ref[s]).astype(BF16)


def dx_rows(pos, d_up, d_lin, w_up, w_lin, part, parts):
    _, tokens, _ = pos.shape
    num_exp, rows, ff = d_up.shape
    width = w_up.shape[1] // parts
    dt = 256
    first = part * (width // dt)
    whole = lambda arr: spec(arr.shape, lambda d: (0,) * arr.ndim)
    w = spec((num_exp, dt, ff), lambda d: (0, first + d, 0))
    o = spec((tokens, dt), lambda d: (0, d))
    full = jax.ShapeDtypeStruct((tokens, width), BF16)
    return call(dx_body, (width // dt,), [whole(pos), whole(d_up), whole(d_lin), w, w], [o, o],
                [full, full], (pos, d_up, d_lin, w_up, w_lin),
                4 * num_exp * rows * ff * width + 4 * tokens * num_exp * (rows // 2) * width,
                [pltpu.VMEM((2, tokens, num_exp * (rows // 2)), BF16), pltpu.VMEM((2, num_exp * (rows // 2), dt), BF16)])


def grads_in_body(xh_ref, xr_ref, ah_ref, ar_ref, bh_ref, br_ref, gu_ref, gl_ref):
    gu_ref[0] = (mm(xh_ref[0], ah_ref[0], TN) + mm(xr_ref[0], ar_ref[0], TN)).astype(BF16)
    gl_ref[0] = (mm(xh_ref[0], bh_ref[0], TN) + mm(xr_ref[0], br_ref[0], TN)).astype(BF16)


def grads_in(x_home, x_rem, da_h, da_r, db_h, db_r):
    num_exp, rows, width = x_home.shape
    ff = da_h.shape[2]
    mt = 1024
    x = spec((1, rows, mt), lambda e, m: (e, 0, m))
    d = spec((1, rows, ff), lambda e, m: (e, 0, 0))
    o = spec((1, mt, ff), lambda e, m: (e, m, 0))
    full = jax.ShapeDtypeStruct((num_exp, width, ff), BF16)
    return call(grads_in_body, (num_exp, width // mt), [x, x, d, d, d, d], [o, o], [full, full],
                (x_home, x_rem, da_h, da_r, db_h, db_r), 8 * num_exp * rows * width * ff)


def grad_down_body(hh_ref, hr_ref, uh_ref, ur_ref, g_ref):
    g_ref[0] = (mm(hh_ref[0], uh_ref[0], TN) + mm(hr_ref[0], ur_ref[0], TN)).astype(BF16)


def grad_down(h_home, h_rem, u_home, u_rem):
    num_exp, rows, ff = h_home.shape
    width = u_home.shape[2]
    mt = 512
    h = spec((1, rows, mt), lambda e, m: (e, 0, m))
    u = spec((1, rows, width), lambda e, m: (e, 0, 0))
    return call(grad_down_body, (num_exp, ff // mt), [h, h, u, u], spec((1, mt, width), lambda e, m: (e, m, 0)),
                jax.ShapeDtypeStruct((num_exp, ff, width), BF16), (h_home, h_rem, u_home, u_rem), 4 * num_exp * rows * width * ff)


def merge_body(*refs, halves, scaled):
    out_ref = refs[-1]
    coef_ref = refs[0] if scaled else None
    ins = list(refs[1:-1] if scaled else refs[:-1])
    width = out_ref.shape[1] // halves
    for k in range(halves):
        total = None
        for n, h in enumerate((1,) * (len(ins) - halves + 1) if halves > 1 else (1,) * len(ins)):
            ref = ins[n + k] if halves > 1 and n == len(ins) - halves else ins[n]
            val = ref[:, k * width:(k + 1) * width] if ref.shape[1] > width else ref[...]
            val = val.astype(F32)
            if scaled:
                val = coef_ref[:, n:n + 1] * val
            total = val if total is None else total + val
        out_ref[:, k * width:(k + 1) * width] = total.astype(BF16)


def merge(arrs, width, part=0, coef=None, halves=1):
    tokens = arrs[0].shape[0]
    rt = 256
    specs = [] if coef is None else [spec((rt, coef.shape[1]), lambda i: (i, 0))]
    for arr in arrs:
        cols = min(arr.shape[1], width)
        specs.append(spec((rt, cols), (lambda i: (i, part)) if arr.shape[1] > cols else (lambda i: (i, 0))))
    args = tuple(arrs) if coef is None else (coef, *arrs)
    return call(functools.partial(merge_body, halves=halves, scaled=coef is not None), (tokens // rt,), specs,
                spec((rt, width), lambda i: (i, 0)), jax.ShapeDtypeStruct((tokens, width), BF16), args, 2 * len(arrs) * tokens * width)


def solution(mesh):
    stages = mesh.shape["stage"]
    groups = mesh.shape["expert"]
    ndev = stages * groups
    tok_spec = P("stage", "expert", None)
    w_spec = P("stage", "expert", None, None)

    def move(arr, step, flip):
        pairs = [(d, ((d // groups + step) % stages) * groups + ((d % groups) ^ flip)) for d in range(ndev)]
        return lax.ppermute(arr, ("stage", "expert"), pairs)

    def device_step(x_act, route_idx, route_gate, w_up, w_lin, w_down, dy_out):
        tokens, width = x_act.shape[1:]
        local_exp = w_up.shape[1]
        num_experts = local_exp * groups
        cap = 4 * tokens // num_experts
        w_up, w_lin, w_down = w_up[0], w_lin[0], w_down[0]
        me = lax.axis_index("expert")

        meta = jnp.concatenate([route_idx[0].astype(F32).T, route_gate[0].T], axis=0)
        metas = jnp.stack([move(meta, 1, flip) for flip in range(groups)])
        ids = metas[:, :2].astype(jnp.int32)
        gates = metas[:, 2:]

        nc = 4
        rows = tokens // nc
        d_own = dy_out[0]
        d_par = move(d_own, 0, 1)
        d_x = [move(d_own[:rows], 0, 2), move(d_own[rows:], 0, 2)]
        d_o = [move(c, 0, 1) for c in d_x]
        x_y = [move(x_act[0, k * rows:(k + 1) * rows], 1, 0) for k in range(nc)]
        x_x = [move(c, 0, 2) for c in x_y]
        x_p = [move(c, 0, 1) for c in x_y]
        x_o = [move(c, 0, 1) for c in x_x]

        exp_ids = me * local_exp + jnp.arange(local_exp, dtype=jnp.int32)
        hit = ids[:, :, None, :] == exp_ids[None, None, :, None]
        member = jnp.any(hit, axis=1)
        lower = (jnp.arange(tokens)[:, None] < jnp.arange(tokens)[None, :]).astype(BF16)
        before = jnp.dot(member.reshape(-1, tokens).astype(BF16), lower, preferred_element_type=F32).astype(jnp.int32).reshape(member.shape)
        pos = jnp.where(member, before, -1)[:, :, None, :]
        sel_gate = jnp.sum(jnp.where(hit, gates[:, :, None, :], 0.0), axis=1)[:, :, None, :]
        here = (ids // local_exp) == me
        there = (ids // local_exp) == (me ^ 1)
        cnt = jnp.sum(here.astype(jnp.int32), axis=1)
        cnt_p = jnp.sum(there.astype(jnp.int32), axis=1)
        two = jnp.sum((cnt == 2).astype(jnp.int32), axis=1)
        both_here = (cnt == 2)[:, None, :]
        pos_any = jnp.where(member, before, -1)
        pos_first = jnp.where(both_here & ~hit[:, 0], -1, pos_any)
        pos_second = jnp.where(both_here & hit[:, 1], before, -1)
        pos_tok = jnp.concatenate([pos_first, pos_second], axis=1).transpose(0, 2, 1)
        pos_col = pos_any.transpose(0, 2, 1)
        gate_here = jnp.sum(jnp.where(here, gates, 0.0), axis=1)
        gate_there = jnp.sum(jnp.where(there, gates, 0.0), axis=1)
        coef = jnp.where((cnt == 2)[:, None], gates, 1.0).transpose(0, 2, 1)
        split = (cnt[2] == 1) & (cnt_p[2] == 1)
        far_coef = jnp.stack([jnp.where(split, gate_here[2], 1.0), jnp.where(split, gate_there[2], 1.0)], axis=1)
        a0 = jnp.where(cnt[0] == 2, 1.0, gate_here[0])
        a1 = jnp.where(cnt_p[0] == 2, 1.0, gate_there[0])
        gate_far = jnp.sum(jnp.where(here[0] | there[0], 0.0, gates[0]), axis=0)
        a2 = jnp.where(cnt[0] + cnt_p[0] == 0, 1.0, gate_far)
        own_coef = jnp.stack([a0, a1, a2], axis=1)

        parts = 2
        half = width // parts
        u_home = dispatch(pos[:2], sel_gate[:2], ([d_own], [d_par]), cap, True)
        x_home = dispatch(pos[:2], sel_gate[:2], (x_y, x_p), cap, False)
        h_h, da_h, db_h = both(x_home, u_home, w_up, w_lin, w_down)

        x_rem = dispatch(pos[2:], sel_gate[2:], (x_x, x_o), cap, False)
        a_r, b_r, h_r = forward(x_rem, w_up, w_lin)
        y_x = []
        for k in range(parts):
            y2, y3 = out_rows(two[2:], pos_tok[2:], coef[2:], h_r, w_down, k, parts)
            y3 = move(y3, 0, 1)
            y_x.append(move(merge([y2, y3], half, coef=far_coef), 0, 2))

        u_rem = dispatch(pos[2:], sel_gate[2:], (d_x, d_o), cap, True)
        da_r, db_r = backward(u_rem, w_down, a_r, b_r)
        dx_x = []
        for k in range(parts):
            r2, r3 = dx_rows(pos_col[2:], da_r, db_r, w_up, w_lin, k, parts)
            r3 = move(r3, 0, 1)
            dx_x.append(move(merge([r2, r3], half), 0, 2))

        r0, r1 = dx_rows(pos_col[:2], da_h, db_h, w_up, w_lin, 0, 1)
        r1 = move(r1, 0, 1)
        dx_out = [move(merge([r0, r1, dx_x[k]], half, part=k), -1, 0) for k in range(parts)]
        dx_prev = jnp.concatenate(dx_out, axis=1)

        y0, y1 = out_rows(two[:2], pos_tok[:2], coef[:2], h_h, w_down, 0, 1)
        y1 = move(y1, 0, 1)
        y_tok = merge([y0, y1, *y_x], width, coef=own_coef, halves=parts)

        g_up, g_lin = grads_in(x_home, x_rem, da_h, da_r, db_h, db_r)
        g_down = grad_down(h_h, h_r, u_home, u_rem)
        return y_tok[None], dx_prev[None], g_up[None], g_lin[None], g_down[None]

    return jax.shard_map(device_step, mesh=mesh, in_specs=(tok_spec, tok_spec, tok_spec, w_spec, w_spec, w_spec, tok_spec), out_specs=(tok_spec, tok_spec, w_spec, w_spec, w_spec), check_vma=False)
```

time: 1050 us -> 717 us (0.68)
  Pallas kernels: 0 us -> 385 us
  matrix products: 384 us -> 0.33 us
  waiting for transfers between devices: 482 us -> 238 us
  local copies, waits for them, and re-layouts: 111 us -> 33.7 us
    all_to_all x4 -> x0, waiting for transfers between devices: 403 us -> none  [the longest x2 207 us: to_experts(): return lax.all_to_all(split_rows, 'expert', 0, 2, tiled=True)[0]]
    pallas_call x0 -> x22, Pallas kernels: none -> 385 us  [call(): pl.pallas_call(body, grid=grid, in_specs=in_specs, out_specs=out_specs, o...]
    dot_general x14 -> x1, matrix products: 384 us -> 0.33 us  [device_step(): jnp.dot(member.reshape(-1, tokens).astype(BF16), lower, preferred_element...]
    ppermute x4 -> x37, waiting for transfers between devices: 79.6 us -> 238 us  [move(): return lax.ppermute(arr, ('stage', 'expert'), pairs)]
    all_to_all x4 -> x0, local copies, waits for them, and re-layouts: 56.2 us -> none  [the longest x2 33.9 us: to_owners(): back_rows = lax.all_to_all(expert_rows[None], 'expert', 2, 0, tiled=True)]
    broadcast_in_dim x2 -> x0, local copies, waits for them, and re-layouts: 44.7 us -> none  [to_owners(): back_rows = lax.all_to_all(expert_rows[None], 'expert', 2, 0, tiled=True)]
    all_to_all x4 -> x0, starting transfers between devices: 28.8 us -> none  [the longest x2 14.6 us: to_experts(): return lax.all_to_all(split_rows, 'expert', 0, 2, tiled=True)[0]]
    ppermute x4 -> x37, starting transfers between devices: 7.39 us -> 27.6 us  [move(): return lax.ppermute(arr, ('stage', 'expert'), pairs)]
  transfers between devices with their start and end apart: 8 -> 37, of which waited for: 5 -> 13; matrix products, arithmetic and copies ran while one was open for 30% -> 7% of each run, Pallas kernels for 0% -> 54%
where the time goes in v1:
time: 717 us; the launch traced here: 712 us
  Pallas kernels  385 us (54%)
  waiting for transfers between devices  238 us (33%)
  local copies, waits for them, and re-layouts  33.7 us (5%)
  starting transfers between devices  27.6 us (4%)
  other arithmetic  27 us (4%)
    pallas_call x22, Pallas kernels, call(): pl.pallas_call(body, grid=grid, in_specs=in_specs, out_specs=out_specs, o...  385 us
    ppermute x37, waiting for transfers between devices, move(): return lax.ppermute(arr, ('stage', 'expert'), pairs)  238 us
    ppermute x37, starting transfers between devices, move(): return lax.ppermute(arr, ('stage', 'expert'), pairs)  27.6 us
  transfers between devices with their start and end apart: 37, of which 13 were waited for; matrix products, arithmetic and copies ran while one was open for 7% of the time, Pallas kernels for 54%

profile of v1, /device:TPU:0, one launch (start us, length us, event | category | flops | bytes accessed | tf_op | source)
XLA Modules:
  0.0 712.4 jit_solution(5094060219498294479)
XLA Ops:
  20.7 20.2 %collective-permute-done = f32[4,1024]{0,1:T(8,128)S(1)} collective-permute-done((f32[4,1024]{0,1:T(8,128)S(1)}, f32[4,1024]{0,1:T(8,128)S(1)}, u32[]{:S(2)}, u32[]{:S(2)}) %collective-permute-start) | collective-permute-done | bytes 16416 | tf_op jit(solution)/shard_map/ppermute | solution.py:299
  82.3 14.8 %collective-permute-done.5.refs_3_ = bf16[256,2048]{1,0:T(8,128)(2,1)} collective-permute-done((bf16[256,2048]{1,0:T(8,128)(2,1)}, bf16[256,2048]{1,0:T(8,128)(2,1)}, u32[]{:S(2)}, u32[]{:S(2)}) %collective-permute-start.5) | collective-permute-done | bytes 1048608 | tf_op jit(solution)/shard_map/ppermute | solution.py:299
  97.2 22.5 %collective-permute-done.6.refs_4_ = bf16[256,2048]{1,0:T(8,128)(2,1)} collective-permute-done((bf16[256,2048]{1,0:T(8,128)(2,1)}, bf16[256,2048]{1,0:T(8,128)(2,1)}, u32[]{:S(2)}, u32[]{:S(2)}) %collective-permute-start.6) | collective-permute-done | bytes 1048608 | tf_op jit(solution)/shard_map/ppermute | solution.py:299
  121.2 20.0 %collective-permute-done.7.refs_5_ = bf16[256,2048]{1,0:T(8,128)(2,1)} collective-permute-done((bf16[256,2048]{1,0:T(8,128)(2,1)}, bf16[256,2048]{1,0:T(8,128)(2,1)}, u32[]{:S(2)}, u32[]{:S(2)}) %collective-permute-start.7) | collective-permute-done | bytes 1048608 | tf_op jit(solution)/shard_map/ppermute | solution.py:299
  147.6 20.0 %collective-permute-done.14.refs_2_ = bf16[256,2048]{1,0:T(8,128)(2,1)} collective-permute-done((bf16[256,2048]{1,0:T(8,128)(2,1)}, bf16[256,2048]{1,0:T(8,128)(2,1)}, u32[]{:S(2)}, u32[]{:S(2)}) %collective-permute-start.14) | collective-permute-done | bytes 1048608 | tf_op jit(solution)/shard_map/ppermute | solution.py:299
  170.2 19.9 %collective-permute-done.15.refs_3_ = bf16[256,2048]{1,0:T(8,128)(2,1)} collective-permute-done((bf16[256,2048]{1,0:T(8,128)(2,1)}, bf16[256,2048]{1,0:T(8,128)(2,1)}, u32[]{:S(2)}, u32[]{:S(2)}) %collective-permute-start.15) | collective-permute-done | bytes 1048608 | tf_op jit(solution)/shard_map/ppermute | solution.py:299
  190.1 22.5 %collective-permute-done.16.refs_4_ = bf16[256,2048]{1,0:T(8,128)(2,1)} collective-permute-done((bf16[256,2048]{1,0:T(8,128)(2,1)}, bf16[256,2048]{1,0:T(8,128)(2,1)}, u32[]{:S(2)}, u32[]{:S(2)}) %collective-permute-start.16) | collective-permute-done | bytes 1048608 | tf_op jit(solution)/shard_map/ppermute | solution.py:299
  212.5 20.8 %collective-permute-done.17.refs_5_ = bf16[256,2048]{1,0:T(8,128)(2,1)} collective-permute-done((bf16[256,2048]{1,0:T(8,128)(2,1)}, bf16[256,2048]{1,0:T(8,128)(2,1)}, u32[]{:S(2)}, u32[]{:S(2)}) %collective-permute-start.17) | collective-permute-done | bytes 1048608 | tf_op jit(solution)/shard_map/ppermute | solution.py:299
  269.2 29.1 %shard_map.115 = (f32[4,512,1024]{2,1,0:T(8,128)}, f32[4,512,1024]{2,1,0:T(8,128)}, bf16[4,512,1024]{2,1,0:T(8,128)(2,1)}) custom-call(bf16[4,512,2048]{2,1,0:T(8,128)(2,1)} %shard_map.114.x_ref.xr_ref, bf16[4,2048,1024]{2,1,0:T(8,128)(2,1)} %bitcast.84, bf16[4,2048,1024]{2,1,0:T(8,128)(2,1)} %bitcast.89), custom_call_target="tpu_custom_call" | custom-call | flops 17179869184 | bytes 41943040 | tf_op jit(solution)/shard_map/pallas_call | solution.py:23
  298.3 13.4 %collective-permute-done.28.refs_3_ = bf16[768,2048]{1,0:T(8,128)(2,1)S(1)} collective-permute-done((bf16[768,2048]{1,0:T(8,128)(2,1)}, bf16[768,2048]{1,0:T(8,128)(2,1)S(1)}, u32[]{:S(2)}, u32[]{:S(2)}) %collective-permute-start.28) | collective-permute-done | bytes 3145760 | tf_op jit(solution)/shard_map/ppermute | solution.py:299
  311.7 15.0 %shard_map.111.u_ref.uh_ref = bf16[4,512,2048]{2,1,0:T(8,128)(2,1)} custom-call(s32[2,4,1,1024]{3,2,1,0:T(1,128)} %copy.72.refs_0_, f32[2,4,1,1024]{3,2,1,0:T(1,128)} %copy.82.refs_1_, bf16[1024,2048]{1,0:T(8,128)(2,1)} %bitcast.21.refs_2_, bf16[1024,2048]{1,0:T(8,128)(2,1)} %collective-permute-done.12.refs_3_), custom_call_target="tpu_custom_call" | custom-call | flops 8589934592 | bytes 8454144 | tf_op jit(solution)/shard_map/pallas_call | solution.py:23
  326.7 37.0 %shard_map.112 = (bf16[4,512,1024]{2,1,0:T(8,128)(2,1)}, bf16[4,512,1024]{2,1,0:T(8,128)(2,1)}, bf16[4,512,1024]{2,1,0:T(8,128)(2,1)}) custom-call(bf16[4,512,2048]{2,1,0:T(8,128)(2,1)} %shard_map.110.x_ref.xh_ref, bf16[4,512,2048]{2,1,0:T(8,128)(2,1)} %shard_map.111.u_ref.uh_ref, bf16[4,2048,1024]{2,1,0:T(8,128)(2,1)} %bitcast.85, ...), custom_call_target="tpu_custom_call" | custom-call | flops 25769803776 | bytes 67108864 | tf_op jit(solution)/shard_map/pallas_call | solution.py:23
  363.6 35.0 %shard_map.121 = (bf16[1024,2048]{1,0:T(8,128)(2,1)}, bf16[1024,2048]{1,0:T(8,128)(2,1)}) custom-call(s32[2,1024,4]{2,1,0:T(8,128)} %get-tuple-element.65.pos_ref, bf16[4,512,1024]{2,1,0:T(8,128)(2,1)} %get-tuple-element.35.da_ref.ah_ref, bf16[4,512,1024]{2,1,0:T(8,128)(2,1)} %get-tuple-element.36.db_ref.bh_ref, bf16[4,2048,1024]{2,1,0:T(8,128)(2,1)} %bitcast.86, ...), custom_call_target="tpu_custom_call" | custom-call | flops 25769803776 | bytes 41975808 | tf_op jit(solution)/shard_map/pallas_call | solution.py:23
  398.7 14.3 %shard_map.122.u_ref.ur_ref = bf16[4,512,2048]{2,1,0:T(8,128)(2,1)} custom-call(s32[2,4,1,1024]{3,2,1,0:T(1,128)} %copy.75.refs_0_, f32[2,4,1,1024]{3,2,1,0:T(1,128)} %copy.83.refs_1_, bf16[256,2048]{1,0:T(8,128)(2,1)} %collective-permute-done.27.refs_2_, bf16[768,2048]{1,0:T(8,128)(2,1)} %copy-done.5, bf16[256,2048]{1,0:T(8,128)(2,1)} %collective-permute-done.29.refs_4_, ...), custom_call_target="tpu_custom_call" | custom-call | flops 8589934592 | bytes 8454144 | tf_op jit(solution)/shard_map/pallas_call | solution.py:23
  413.0 22.4 %shard_map.123 = (bf16[4,512,1024]{2,1,0:T(8,128)(2,1)}, bf16[4,512,1024]{2,1,0:T(8,128)(2,1)}) custom-call(bf16[4,512,2048]{2,1,0:T(8,128)(2,1)} %shard_map.122.u_ref.ur_ref, bf16[4,1024,2048]{2,1,0:T(8,128)(2,1)} %bitcast.72, f32[4,512,1024]{2,1,0:T(8,128)} %get-tuple-element.39.a_ref, f32[4,512,1024]{2,1,0:T(8,128)} %get-tuple-element.40.b_ref), custom_call_target="tpu_custom_call" | custom-call | flops 8589934592 | bytes 41943040 | tf_op jit(solution)/shard_map/pallas_call | solution.py:23
  435.4 21.0 %shard_map.127 = (bf16[1024,1024]{1,0:T(8,128)(2,1)}, bf16[1024,1024]{1,0:T(8,128)(2,1)}) custom-call(s32[2,1024,4]{2,1,0:T(8,128)} %get-tuple-element.64.pos_ref, bf16[4,512,1024]{2,1,0:T(8,128)(2,1)} %get-tuple-element.41.da_ref.ar_ref, bf16[4,512,1024]{2,1,0:T(8,128)(2,1)} %get-tuple-element.42.db_ref.br_ref, bf16[4,2048,1024]{2,1,0:T(8,128)(2,1)} %bitcast.87, ...), custom_call_target="tpu_custom_call" | custom-call | flops 12884901888 | bytes 41975808 | tf_op jit(solution)/shard_map/pallas_call | solution.py:23
  456.4 21.0 %shard_map.124 = (bf16[1024,1024]{1,0:T(8,128)(2,1)}, bf16[1024,1024]{1,0:T(8,128)(2,1)}) custom-call(s32[2,1024,4]{2,1,0:T(8,128)} %get-tuple-element.64.pos_ref, bf16[4,512,1024]{2,1,0:T(8,128)(2,1)} %get-tuple-element.41.da_ref.ar_ref, bf16[4,512,1024]{2,1,0:T(8,128)(2,1)} %get-tuple-element.42.db_ref.br_ref, bf16[4,2048,1024]{2,1,0:T(8,128)(2,1)} %bitcast.88, ...), custom_call_target="tpu_custom_call" | custom-call | flops 12884901888 | bytes 41975808 | tf_op jit(solution)/shard_map/pallas_call | solution.py:23
  477.9 16.9 %shard_map.116 = (bf16[1024,1024]{1,0:T(8,128)(2,1)}, bf16[1024,1024]{1,0:T(8,128)(2,1)}) custom-call(s32[2]{0:T(128)} %get-tuple-element.82.two_ref, s32[2,1024,8]{2,1,0:T(8,128)} %get-tuple-element.72.pos_ref, f32[2,1024,2]{2,1,0:T(8,128)} %get-tuple-element.70.coef_ref, bf16[4,512,1024]{2,1,0:T(8,128)(2,1)} %get-tuple-element.30.h_ref.hr_ref, ...), custom_call_target="tpu_custom_call" | custom-call | flops 12884901888 | bytes 21053448 | tf_op jit(solution)/shard_map/pallas_call | solution.py:23
  495.3 16.5 %shard_map.118 = (bf16[1024,1024]{1,0:T(8,128)(2,1)}, bf16[1024,1024]{1,0:T(8,128)(2,1)}) custom-call(s32[2]{0:T(128)} %get-tuple-element.82.two_ref, s32[2,1024,8]{2,1,0:T(8,128)} %get-tuple-element.72.pos_ref, f32[2,1024,2]{2,1,0:T(8,128)} %get-tuple-element.70.coef_ref, bf16[4,512,1024]{2,1,0:T(8,128)(2,1)} %get-tuple-element.30.h_ref.hr_ref, ...), custom_call_target="tpu_custom_call" | custom-call | flops 12884901888 | bytes 21053448 | tf_op jit(solution)/shard_map/pallas_call | solution.py:23
  523.9 27.6 %shard_map.113 = (bf16[1024,2048]{1,0:T(8,128)(2,1)}, bf16[1024,2048]{1,0:T(8,128)(2,1)}) custom-call(s32[2]{0:T(128)} %get-tuple-element.83.two_ref, s32[2,1024,8]{2,1,0:T(8,128)} %get-tuple-element.73.pos_ref, f32[2,1024,2]{2,1,0:T(8,128)} %get-tuple-element.71.coef_ref, bf16[4,512,1024]{2,1,0:T(8,128)(2,1)} %get-tuple-element.27.h_ref.hh_ref, ...), custom_call_target="tpu_custom_call" | custom-call | flops 25769803776 | bytes 21053448 | tf_op jit(solution)/shard_map/pallas_call | solution.py:23
  571.4 38.6 %collective-permute-done.32.refs_2_ = bf16[1024,1024]{1,0:T(8,128)(2,1)} collective-permute-done((bf16[1024,1024]{1,0:T(8,128)(2,1)}, bf16[1024,1024]{1,0:T(8,128)(2,1)}, u32[]{:S(2)}, u32[]{:S(2)}) %collective-permute-start.32) | collective-permute-done | bytes 2097184 | tf_op jit(solution)/shard_map/ppermute | solution.py:299
  616.3 40.9 %shard_map.130 = (bf16[4,2048,1024]{2,1,0:T(8,128)(2,1)}, bf16[4,2048,1024]{2,1,0:T(8,128)(2,1)}) custom-call(bf16[4,512,2048]{2,1,0:T(8,128)(2,1)} %shard_map.110.x_ref.xh_ref, bf16[4,512,2048]{2,1,0:T(8,128)(2,1)} %shard_map.114.x_ref.xr_ref, bf16[4,512,1024]{2,1,0:T(8,128)(2,1)} %get-tuple-element.35.da_ref.ah_ref, ...), custom_call_target="tpu_custom_call" | custom-call | flops 34359738368 | bytes 33554432 | tf_op jit(solution)/shard_map/pallas_call | solution.py:23
  657.3 25.9 %shard_map.131 = bf16[4,1024,2048]{2,1,0:T(8,128)(2,1)} custom-call(bf16[4,512,1024]{2,1,0:T(8,128)(2,1)} %get-tuple-element.27.h_ref.hh_ref, bf16[4,512,1024]{2,1,0:T(8,128)(2,1)} %get-tuple-element.30.h_ref.hr_ref, bf16[4,512,2048]{2,1,0:T(8,128)(2,1)} %shard_map.111.u_ref.uh_ref, bf16[4,512,2048]{2,1,0:T(8,128)(2,1)} %shard_map.122.u_ref.ur_ref), custom_call_target="tpu_custom_call" | custom-call | flops 17179869184 | bytes 25165824 | tf_op jit(solution)/shard_map/pallas_call | solution.py:23
  683.2 16.2 %collective-permute-done.25.refs_4_ = bf16[1024,1024]{1,0:T(8,128)(2,1)} collective-permute-done((bf16[1024,1024]{1,0:T(8,128)(2,1)}, bf16[1024,1024]{1,0:T(8,128)(2,1)}, u32[]{:S(2)}, u32[]{:S(2)}) %collective-permute-start.25) | collective-permute-done | bytes 2097184 | tf_op jit(solution)/shard_map/ppermute | solution.py:299
  (134 shorter events, 159.8 us)
Async XLA Ops:
  12.7 69.1 %collective-permute-start.4 = (bf16[256,2048]{1,0:T(8,128)(2,1)}, bf16[256,2048]{1,0:T(8,128)(2,1)}, u32[]{:S(2)}, u32[]{:S(2)}) collective-permute-start(bf16[256,2048]{1,0:T(8,128)(2,1)} %get-tuple-element.61), channel_id=1, source_target_pairs={{0,4},{1,5},{2,6},{3,7},{4,0},{5,1},{6,2},{7,3}} | collective-permute-start | bytes 3145736 | tf_op jit(solution)/shard_map/ppermute | solution.py:299
  40.9 56.3 %collective-permute-start.5 = (bf16[256,2048]{1,0:T(8,128)(2,1)}, bf16[256,2048]{1,0:T(8,128)(2,1)}, u32[]{:S(2)}, u32[]{:S(2)}) collective-permute-start(bf16[256,2048]{1,0:T(8,128)(2,1)} %get-tuple-element.60), channel_id=1, source_target_pairs={{0,4},{1,5},{2,6},{3,7},{4,0},{5,1},{6,2},{7,3}} | collective-permute-start | bytes 3145736 | tf_op jit(solution)/shard_map/ppermute | solution.py:299
  42.9 76.7 %collective-permute-start.6 = (bf16[256,2048]{1,0:T(8,128)(2,1)}, bf16[256,2048]{1,0:T(8,128)(2,1)}, u32[]{:S(2)}, u32[]{:S(2)}) collective-permute-start(bf16[256,2048]{1,0:T(8,128)(2,1)} %get-tuple-element.62), channel_id=1, source_target_pairs={{0,4},{1,5},{2,6},{3,7},{4,0},{5,1},{6,2},{7,3}} | collective-permute-start | bytes 3145736 | tf_op jit(solution)/shard_map/ppermute | solution.py:299
  42.9 98.3 %collective-permute-start.7 = (bf16[256,2048]{1,0:T(8,128)(2,1)}, bf16[256,2048]{1,0:T(8,128)(2,1)}, u32[]{:S(2)}, u32[]{:S(2)}) collective-permute-start(bf16[256,2048]{1,0:T(8,128)(2,1)} %get-tuple-element.59), channel_id=1, source_target_pairs={{0,4},{1,5},{2,6},{3,7},{4,0},{5,1},{6,2},{7,3}} | collective-permute-start | bytes 3145736 | tf_op jit(solution)/shard_map/ppermute | solution.py:299
  51.6 91.3 %collective-permute-start.27 = (bf16[256,2048]{1,0:T(8,128)(2,1)}, bf16[256,2048]{1,0:T(8,128)(2,1)}, u32[]{:S(2)}, u32[]{:S(2)}) collective-permute-start(bf16[256,2048]{1,0:T(8,128)(2,1)} %slice_bitcast_fusion.6), channel_id=1, source_target_pairs={{0,2},{1,3},{2,0},{3,1},{4,6},{5,7},{6,4},{7,5}} | collective-permute-start | bytes 3145736 | tf_op jit(solution)/shard_map/ppermute | solution.py:299
  81.8 62.7 %collective-permute-start.8 = (bf16[256,2048]{1,0:T(8,128)(2,1)}, bf16[256,2048]{1,0:T(8,128)(2,1)S(1)}, u32[]{:S(2)}, u32[]{:S(2)}) collective-permute-start(bf16[256,2048]{1,0:T(8,128)(2,1)} %collective-permute-done.4.refs_2_), channel_id=1, source_target_pairs={{0,1},{1,0},{2,3},{3,2},{4,5},{5,4},{6,7},{7,6}} | collective-permute-start | bytes 3145736 | tf_op jit(solution)/shard_map/ppermute | solution.py:299
  97.2 47.6 %collective-permute-start.9 = (bf16[256,2048]{1,0:T(8,128)(2,1)}, bf16[256,2048]{1,0:T(8,128)(2,1)S(1)}, u32[]{:S(2)}, u32[]{:S(2)}) collective-permute-start(bf16[256,2048]{1,0:T(8,128)(2,1)} %collective-permute-done.5.refs_3_), channel_id=1, source_target_pairs={{0,1},{1,0},{2,3},{3,2},{4,5},{5,4},{6,7},{7,6}} | collective-permute-start | bytes 3145736 | tf_op jit(solution)/shard_map/ppermute | solution.py:299
  144.8 67.7 %collective-permute-start.16 = (bf16[256,2048]{1,0:T(8,128)(2,1)}, bf16[256,2048]{1,0:T(8,128)(2,1)}, u32[]{:S(2)}, u32[]{:S(2)}) collective-permute-start(bf16[256,2048]{1,0:T(8,128)(2,1)} %collective-permute-done.6.refs_4_), channel_id=1, source_target_pairs={{0,2},{1,3},{2,0},{3,1},{4,6},{5,7},{6,4},{7,5}} | collective-permute-start | bytes 3145736 | tf_op jit(solution)/shard_map/ppermute | solution.py:299
  146.5 86.8 %collective-permute-start.17 = (bf16[256,2048]{1,0:T(8,128)(2,1)}, bf16[256,2048]{1,0:T(8,128)(2,1)}, u32[]{:S(2)}, u32[]{:S(2)}) collective-permute-start(bf16[256,2048]{1,0:T(8,128)(2,1)} %collective-permute-done.7.refs_5_), channel_id=1, source_target_pairs={{0,2},{1,3},{2,0},{3,1},{4,6},{5,7},{6,4},{7,5}} | collective-permute-start | bytes 3145736 | tf_op jit(solution)/shard_map/ppermute | solution.py:299
  147.5 164.1 %collective-permute-start.12 = (bf16[1024,2048]{1,0:T(8,128)(2,1)}, bf16[1024,2048]{1,0:T(8,128)(2,1)}, u32[]{:S(2)}, u32[]{:S(2)}) collective-permute-start(bf16[1024,2048]{1,0:T(8,128)(2,1)} %bitcast.21.refs_2_), channel_id=1, source_target_pairs={{0,1},{1,0},{2,3},{3,2},{4,5},{5,4},{6,7},{7,6}} | collective-permute-start | bytes 12582920 | tf_op jit(solution)/shard_map/ppermute | solution.py:299
  167.6 73.4 %collective-permute-start.18 = (bf16[256,2048]{1,0:T(8,128)(2,1)}, bf16[256,2048]{1,0:T(8,128)(2,1)}, u32[]{:S(2)}, u32[]{:S(2)}) collective-permute-start(bf16[256,2048]{1,0:T(8,128)(2,1)} %collective-permute-done.14.refs_2_), channel_id=1, source_target_pairs={{0,1},{1,0},{2,3},{3,2},{4,5},{5,4},{6,7},{7,6}} | collective-permute-start | bytes 3145736 | tf_op jit(solution)/shard_map/ppermute | solution.py:299
  190.1 65.5 %collective-permute-start.19 = (bf16[256,2048]{1,0:T(8,128)(2,1)}, bf16[256,2048]{1,0:T(8,128)(2,1)}, u32[]{:S(2)}, u32[]{:S(2)}) collective-permute-start(bf16[256,2048]{1,0:T(8,128)(2,1)} %collective-permute-done.15.refs_3_), channel_id=1, source_target_pairs={{0,1},{1,0},{2,3},{3,2},{4,5},{5,4},{6,7},{7,6}} | collective-permute-start | bytes 3145736 | tf_op jit(solution)/shard_map/ppermute | solution.py:299
  241.0 70.7 %collective-permute-start.28 = (bf16[768,2048]{1,0:T(8,128)(2,1)}, bf16[768,2048]{1,0:T(8,128)(2,1)S(1)}, u32[]{:S(2)}, u32[]{:S(2)}) collective-permute-start(bf16[768,2048]{1,0:T(8,128)(2,1)} %slice_bitcast_fusion), channel_id=1, source_target_pairs={{0,2},{1,3},{2,0},{3,1},{4,6},{5,7},{6,4},{7,5}} | collective-permute-start | bytes 9437192 | tf_op jit(solution)/shard_map/ppermute | solution.py:299
  255.6 143.1 %collective-permute-start.29 = (bf16[256,2048]{1,0:T(8,128)(2,1)}, bf16[256,2048]{1,0:T(8,128)(2,1)}, u32[]{:S(2)}, u32[]{:S(2)}) collective-permute-start(bf16[256,2048]{1,0:T(8,128)(2,1)} %collective-permute-done.27.refs_2_), channel_id=1, source_target_pairs={{0,1},{1,0},{2,3},{3,2},{4,5},{5,4},{6,7},{7,6}} | collective-permute-start | bytes 3145736 | tf_op jit(solution)/shard_map/ppermute | solution.py:299
  311.7 87.0 %collective-permute-start.30 = (bf16[768,2048]{1,0:T(8,128)(2,1)S(1)}, bf16[768,2048]{1,0:T(8,128)(2,1)}, u32[]{:S(2)}, u32[]{:S(2)}) collective-permute-start(bf16[768,2048]{1,0:T(8,128)(2,1)S(1)} %collective-permute-done.28.refs_3_), channel_id=1, source_target_pairs={{0,1},{1,0},{2,3},{3,2},{4,5},{5,4},{6,7},{7,6}} | collective-permute-start | bytes 9437192 | tf_op jit(solution)/shard_map/ppermute | solution.py:299
  398.6 163.7 %collective-permute-start.26 = (bf16[1024,2048]{1,0:T(8,128)(2,1)}, bf16[1024,2048]{1,0:T(8,128)(2,1)}, u32[]{:S(2)}, u32[]{:S(2)}) collective-permute-start(bf16[1024,2048]{1,0:T(8,128)(2,1)} %get-tuple-element.38), channel_id=1, source_target_pairs={{0,1},{1,0},{2,3},{3,2},{4,5},{5,4},{6,7},{7,6}} | collective-permute-start | bytes 12582920 | tf_op jit(solution)/shard_map/ppermute | solution.py:299
  494.9 56.6 %collective-permute-start.22 = (bf16[1024,1024]{1,0:T(8,128)(2,1)}, bf16[1024,1024]{1,0:T(8,128)(2,1)}, u32[]{:S(2)}, u32[]{:S(2)}) collective-permute-start(bf16[1024,1024]{1,0:T(8,128)(2,1)} %get-tuple-element.32), channel_id=1, source_target_pairs={{0,1},{1,0},{2,3},{3,2},{4,5},{5,4},{6,7},{7,6}} | collective-permute-start | bytes 6291464 | tf_op jit(solution)/shard_map/ppermute | solution.py:299
  516.2 48.8 %collective-permute-start.35 = (bf16[1024,1024]{1,0:T(8,128)(2,1)}, bf16[1024,1024]{1,0:T(8,128)(2,1)}, u32[]{:S(2)}, u32[]{:S(2)}) collective-permute-start(bf16[1024,1024]{1,0:T(8,128)(2,1)} %shard_map.128), channel_id=1, source_target_pairs={{0,2},{1,3},{2,0},{3,1},{4,6},{5,7},{6,4},{7,5}} | collective-permute-start | bytes 6291464 | tf_op jit(solution)/shard_map/ppermute | solution.py:299
  523.3 86.7 %collective-permute-start.32 = (bf16[1024,1024]{1,0:T(8,128)(2,1)}, bf16[1024,1024]{1,0:T(8,128)(2,1)}, u32[]{:S(2)}, u32[]{:S(2)}) collective-permute-start(bf16[1024,1024]{1,0:T(8,128)(2,1)} %shard_map.125), channel_id=1, source_target_pairs={{0,2},{1,3},{2,0},{3,1},{4,6},{5,7},{6,4},{7,5}} | collective-permute-start | bytes 6291464 | tf_op jit(solution)/shard_map/ppermute | solution.py:299
  551.5 147.9 %collective-permute-start.13 = (bf16[1024,2048]{1,0:T(8,128)(2,1)}, bf16[1024,2048]{1,0:T(8,128)(2,1)}, u32[]{:S(2)}, u32[]{:S(2)}) collective-permute-start(bf16[1024,2048]{1,0:T(8,128)(2,1)} %get-tuple-element.29), channel_id=1, source_target_pairs={{0,1},{1,0},{2,3},{3,2},{4,5},{5,4},{6,7},{7,6}} | collective-permute-start | bytes 12582920 | tf_op jit(solution)/shard_map/ppermute | solution.py:299
  556.2 127.0 %collective-permute-start.23 = (bf16[1024,1024]{1,0:T(8,128)(2,1)}, bf16[1024,1024]{1,0:T(8,128)(2,1)S(1)}, u32[]{:S(2)}, u32[]{:S(2)}) collective-permute-start(bf16[1024,1024]{1,0:T(8,128)(2,1)} %shard_map.117), channel_id=1, source_target_pairs={{0,2},{1,3},{2,0},{3,1},{4,6},{5,7},{6,4},{7,5}} | collective-permute-start | bytes 6291464 | tf_op jit(solution)/shard_map/ppermute | solution.py:299
  562.4 137.0 %collective-permute-start.25 = (bf16[1024,1024]{1,0:T(8,128)(2,1)}, bf16[1024,1024]{1,0:T(8,128)(2,1)}, u32[]{:S(2)}, u32[]{:S(2)}) collective-permute-start(bf16[1024,1024]{1,0:T(8,128)(2,1)} %shard_map.119), channel_id=1, source_target_pairs={{0,2},{1,3},{2,0},{3,1},{4,6},{5,7},{6,4},{7,5}} | collective-permute-start | bytes 6291464 | tf_op jit(solution)/shard_map/ppermute | solution.py:299
  569.9 137.5 %collective-permute-start.36 = (bf16[1024,1024]{1,0:T(8,128)(2,1)}, bf16[1024,1024]{1,0:T(8,128)(2,1)}, u32[]{:S(2)}, u32[]{:S(2)}) collective-permute-start(bf16[1024,1024]{1,0:T(8,128)(2,1)} %shard_map.129), channel_id=1, source_target_pairs={{0,4},{1,5},{2,6},{3,7},{4,0},{5,1},{6,2},{7,3}} | collective-permute-start | bytes 6291464 | tf_op jit(solution)/shard_map/ppermute | solution.py:299
  614.9 92.5 %collective-permute-start.33 = (bf16[1024,1024]{1,0:T(8,128)(2,1)}, bf16[1024,1024]{1,0:T(8,128)(2,1)}, u32[]{:S(2)}, u32[]{:S(2)}) collective-permute-start(bf16[1024,1024]{1,0:T(8,128)(2,1)} %shard_map.126), channel_id=1, source_target_pairs={{0,4},{1,5},{2,6},{3,7},{4,0},{5,1},{6,2},{7,3}} | collective-permute-start | bytes 6291464 | tf_op jit(solution)/shard_map/ppermute | solution.py:299
  (23 other events, 521.6 us)
